TPU v7x, 32 devices: a whole 2x2x4 slice. The times are simulated.
32 devices in a mesh: seq: 8 (over y, x, core), head: 4 (over z).
Axes of the slice: x: 2, y: 2, z: 4, core: 2. Of those that a mesh axis runs over, the one named last changes fastest.
Arguments:
- segment_input: bfloat16 [2, 2048, 3584], P(None, 'seq'), may hold values from -16 to 16
- doc_ids: int32 [2, 2048], replicated, may hold values from 0 to 3, never falling along the last dimension, each value on 1 to 1024 neighbouring positions
- memory: bfloat16 [32, 3584], replicated, may hold values from -16 to 16
- gain: bfloat16 [3584], replicated, may hold values from 0.099609375 to 1.8984375
- w_query: bfloat16 [3584, 4096], P(None, 'head'), may hold values from -4 to 4
- w_key: bfloat16 [3584, 2048], P(None, 'head'), may hold values from -4 to 4
- w_value: bfloat16 [3584, 2048], P(None, 'head'), may hold values from -0.09375 to 0.09375
- w_out: bfloat16 [4096, 3584], P(None, 'head'), may hold values from -0.09375 to 0.09375
- mem_proj: bfloat16 [3584, 3584], P('head'), may hold values from -4 to 4
Outputs:
- hidden: bfloat16 [2, 2048, 3584], P(None, 'seq', 'head')
- new_memory: bfloat16 [32, 3584], replicated
Inputs may be any that keep to these rules, and one draw needn't show every extreme that they name: `doc_ids`: ids never fall along a segment; each document has 1 to 1024 tokens.
All inputs are finite; a program needn't handle non-finite values.
Results may differ from a plain program's by a relative error of at most 0.02.
Values may be sent and summed in bfloat16 or wider, within the bound.
A program may use at most 128 MiB of HBM per device.

v0:
```python
import jax
import jax.numpy as jnp
from jax import lax
from jax.sharding import PartitionSpec as P

HD = 256


def rms_norm(rows, gain):
    values = rows.astype(jnp.float32)
    scaled = values * lax.rsqrt(jnp.mean(values * values, axis=-1, keepdims=True) + 1e-06)
    return (scaled * gain.astype(jnp.float32)).astype(jnp.bfloat16)


def combine(first, second):
    peak = jnp.maximum(first[0], second[0])
    left = jnp.exp(first[0] - peak)
    right = jnp.exp(second[0] - peak)
    return (
        peak,
        first[1] * left + second[1] * right,
        first[2] * left[..., None] + second[2] * right[..., None],
    )


def partial_block(query, keys, values, valid):
    scale = jnp.float32(HD ** (-0.5))
    key_heads = keys.reshape(keys.shape[0], -1, HD)
    value_heads = values.reshape(values.shape[0], -1, HD)
    scores = (
        jnp.einsum("rhgd,khd->hgrk", query, key_heads, preferred_element_type=jnp.float32) * scale
    )
    scores = jnp.where(valid[None, None], scores, -1e30)
    peak = jnp.max(scores, axis=-1)
    weights = jnp.where(valid[None, None], jnp.exp(scores - peak[..., None]), 0.0)
    total = jnp.sum(weights, axis=-1)
    mixed = jnp.einsum(
        "hgrk,khd->hgrd",
        weights.astype(jnp.bfloat16),
        value_heads,
        preferred_element_type=jnp.float32,
    )
    return (peak, total, mixed)


def finish(state):
    mixed = state[2] / state[1][..., None]
    return mixed.transpose(2, 0, 1, 3).reshape(mixed.shape[2], -1).astype(jnp.bfloat16)


def per_device(segment_input, doc_ids, memory, gain, w_query, w_key, w_value, w_out, mem_proj):
    tok_rows = segment_input.shape[1]
    columns = w_out.shape[1]
    kv_local = w_key.shape[1] // HD
    col_start = lax.axis_index("head") * columns
    row_start = lax.axis_index("seq") * tok_rows
    my_pos = row_start + jnp.arange(tok_rows, dtype=jnp.int32)
    mem = memory
    outputs = []
    for seg in range(segment_input.shape[0]):
        tokens = segment_input[seg]
        docs = doc_ids[seg]
        my_docs = lax.dynamic_slice_in_dim(docs, row_start, tok_rows, 0)
        normed_x = rms_norm(tokens, gain)
        normed_m = rms_norm(mem, gain)
        query = (
            jnp.dot(normed_x, w_query, preferred_element_type=jnp.float32)
            .astype(jnp.bfloat16)
            .reshape(tok_rows, kv_local, 2, HD)
        )
        keys = jnp.dot(normed_x, w_key, preferred_element_type=jnp.float32).astype(jnp.bfloat16)
        values = jnp.dot(normed_x, w_value, preferred_element_type=jnp.float32).astype(jnp.bfloat16)
        mem_query = (
            jnp.dot(normed_m, w_query, preferred_element_type=jnp.float32)
            .astype(jnp.bfloat16)
            .reshape(mem.shape[0], kv_local, 2, HD)
        )
        mem_keys = jnp.dot(normed_m, w_key, preferred_element_type=jnp.float32).astype(jnp.bfloat16)
        mem_values = jnp.dot(normed_m, w_value, preferred_element_type=jnp.float32).astype(
            jnp.bfloat16
        )
        open_tok = jnp.ones((tok_rows, mem.shape[0]), dtype=bool)
        open_mem = jnp.ones((mem.shape[0], mem.shape[0]), dtype=bool)
        tok_init = partial_block(query, mem_keys, mem_values, open_tok)
        mem_init = partial_block(mem_query, mem_keys, mem_values, open_mem)
        both_pieces = (
            lax.all_gather(keys, "seq", axis=0, tiled=True),
            lax.all_gather(values, "seq", axis=0, tiled=True),
        )
        open_keys = jnp.ones((mem.shape[0], both_pieces[0].shape[0]), dtype=bool)
        written = combine(
            mem_init, partial_block(mem_query, both_pieces[0], both_pieces[1], open_keys)
        )
        key_piece, value_piece = both_pieces
        key_pos = jnp.arange(key_piece.shape[0], dtype=jnp.int32)
        valid = (key_pos[None, :] <= my_pos[:, None]) & (docs[None, :] == my_docs[:, None])
        tok_state = combine(tok_init, partial_block(query, key_piece, value_piece, valid))
        attn_tok = finish(tok_state)
        attn_mem = finish(written)
        out_tok = jnp.dot(
            lax.all_gather(attn_tok, "head", axis=1, tiled=True),
            w_out,
            preferred_element_type=jnp.float32,
        )
        out_mem = jnp.dot(
            lax.all_gather(attn_mem, "head", axis=1, tiled=True),
            w_out,
            preferred_element_type=jnp.float32,
        )
        token_cols = lax.dynamic_slice_in_dim(tokens, col_start, columns, 1).astype(jnp.float32)
        outputs.append((token_cols + out_tok).astype(jnp.bfloat16))
        mem_cols = lax.dynamic_slice_in_dim(mem, col_start, columns, 1).astype(jnp.float32)
        mem_out = (mem_cols + out_mem).astype(jnp.bfloat16)
        partial_mem = jnp.dot(mem_out, mem_proj, preferred_element_type=jnp.float32)
        mem = lax.psum(partial_mem.astype(jnp.bfloat16), "head")
    return (jnp.stack(outputs, axis=0), mem)


def solution(mesh):
    return jax.shard_map(
        per_device,
        mesh=mesh,
        in_specs=(
            P(None, "seq", None),
            P(),
            P(),
            P(),
            P(None, "head"),
            P(None, "head"),
            P(None, "head"),
            P(None, "head"),
            P("head", None),
        ),
        out_specs=(P(None, "seq", "head"), P()),
        check_vma=False,
    )
```

profile of v0, /device:TPU:0, one launch (start us, length us, event | category | flops | bytes accessed | tf_op | source)
XLA Modules:
  0.0 315.8 jit_solution(6064854172104741150)
XLA Ops:
  7.2 0.9 convert_element_type.159
  8.1 3.0 fusion.12
  11.1 3.9 %convolution_convert_fusion.7 = bf16[256,512]{1,0:T(8,128)(2,1)} fusion(bf16[3584,512]{1,0:T(8,128)(2,1)} %param.14, f32[3584]{0:T(1024)S(1)} %convert_element_type.159, f32[256]{0:T(256)S(1)} %add_rsqrt_fusion.1, bf16[2,256,3584]{2,1,0:T(8,128)(2,1)S(1)} %copy-done), kind=kOutput, calls=%fused_computation.64 | convolution fusion | flops 943325184 | bytes 5784576 | tf_op jit(solution)/shard_map/dot_general | solution.py:71
  15.1 4.5 %convolution_convert_fusion.6 = bf16[256,512]{1,0:T(8,128)(2,1)} fusion(bf16[3584,512]{1,0:T(8,128)(2,1)} %param.15, f32[3584]{0:T(1024)S(1)} %convert_element_type.159, f32[256]{0:T(256)S(1)} %add_rsqrt_fusion.1, bf16[2,256,3584]{2,1,0:T(8,128)(2,1)} %param.9), kind=kOutput, calls=%fused_computation.63 | convolution fusion | flops 943325184 | bytes 5782528 | tf_op jit(solution)/shard_map/dot_general | solution.py:72
  19.7 4.5 %convolution_convert_fusion.5 = bf16[256,512]{1,0:T(8,128)(2,1)} fusion(bf16[3584,512]{1,0:T(8,128)(2,1)} %param.14, f32[256]{0:T(256)S(1)} %add_rsqrt_fusion, f32[3584]{0:T(1024)S(1)} %convert_element_type.159, bf16[2,256,3584]{2,1,0:T(8,128)(2,1)} %param.9), kind=kOutput, calls=%fused_computation.62 | convolution fusion | flops 943325184 | bytes 5782528 | tf_op jit(solution)/shard_map/dot_general | solution.py:71
  24.2 4.7 %convolution_convert_fusion.4 = bf16[256,512]{1,0:T(8,128)(2,1)} fusion(bf16[3584,512]{1,0:T(8,128)(2,1)} %param.15, f32[256]{0:T(256)S(1)} %add_rsqrt_fusion, f32[3584]{0:T(1024)S(1)} %convert_element_type.159, bf16[2,256,3584]{2,1,0:T(8,128)(2,1)} %param.9), kind=kOutput, calls=%fused_computation.61 | convolution fusion | flops 943325184 | bytes 5782528 | tf_op jit(solution)/shard_map/dot_general | solution.py:72
  29.4 3.0 convolution_convert_fusion.13
  33.2 4.8 %convolution_convert_fusion.9 = bf16[32,1024]{1,0:T(8,128)(2,1)S(1)} fusion(bf16[3584,1024]{1,0:T(8,128)(2,1)} %param.13, bf16[32,3584]{1,0:T(8,128)(2,1)S(1)} %copy-done.7, f32[3584]{0:T(1024)S(1)} %convert_element_type.159, f32[32]{0:T(128)S(1)} %add_rsqrt_fusion.3), kind=kOutput, calls=%fused_computation.86 | convolution fusion | flops 235372544 | bytes 7649408 | tf_op jit(solution)/shard_map/dot_general | solution.py:74
  38.2 2.2 convolution_convert_fusion.3
  40.4 2.2 convolution_convert_fusion.2
  43.6 1.2 reshape.316
  46.0 2.3 fusion.21
  48.3 2.6 reshape.312
  50.9 1.4 fusion.160
  52.4 23.1 %all-gather.9.cloned.1.call-done = bf16[2048,512]{1,0:T(8,128)(2,1)} async-done(((bf16[256,512]{1,0:T(8,128)(2,1)}), bf16[2048,512]{1,0:T(8,128)(2,1)}) %all-gather.9.cloned.1.call-update) | async-done | bytes 2097168 | tf_op jit(solution)/shard_map/all_gather | solution.py:88
  75.4 4.0 %reshape.313 = bf16[2048,2,256]{2,1,0:T(2,128)(2,1)} reshape(bf16[2048,512]{1,0:T(8,128)(2,1)} %all-gather.9.cloned.1.call-done) | data formatting | bytes 4194304 | tf_op jit(solution)/shard_map/reshape | solution.py:29
  79.4 4.7 %copy.73 = bf16[2048,2,256,1]{0,2,3,1:T(8,128)(2,1)S(1)} copy(bf16[2048,2,256,1]{2,1,0,3:T(2,128)(2,1)} %bitcast.248) | data formatting | bytes 4194304 | tf_op jit(solution)/shard_map/reshape | solution.py:29
  85.6 14.1 %all_gather.27 = bf16[32,4096]{1,0:T(8,128)(2,1)S(1)} all-gather(bf16[32,1024]{1,0:T(8,128)(2,1)S(1)} %convert_element_type.181), channel_id=1, replica_groups=mesh['seq'=8,'head'=4] {'head'}, dimensions={1}, use_global_device_ids=true | all-gather | bytes 327680 | tf_op jit(solution)/shard_map/all_gather | solution.py:106
  99.7 3.5 %fusion = (f32[2,2,256]{2,1,0:T(2,128)S(1)}, f32[2,2048,256,2]{2,1,3,0:T(8,128)S(1)}) fusion(pred[256,2048]{0,1:T(8,128)(4,1)} %get-tuple-element.20, bf16[256,2,2,256]{3,2,1,0:T(2,128)(2,1)} %copy-done.12, bf16[2048,2,256,1]{2,1,0,3:T(2,128)(2,1)} %bitcast.247), kind=kOutput, calls=%fused_computation.4 | convolution fusion | flops 1080032256 | bytes 11538432 | tf_op jit(solution)/shard_map/rhgd,khd->hgrk/dot_general | solution.py:31
  103.3 2.1 fusion.2
  105.4 1.1 copy-done.4
  106.5 8.0 %convolution_convert_fusion.1 = bf16[32,3584]{1,0:T(8,128)(2,1)} fusion(bf16[896,3584]{1,0:T(8,128)(2,1)} %param.17, bf16[32,4096]{1,0:T(8,128)(2,1)S(1)} %all_gather.27, bf16[4096,896]{1,0:T(8,128)(2,1)} %param.16, bf16[32,3584]{1,0:T(8,128)(2,1)S(1)} %copy-done.7, s32[]{:T(128)S(6)} %select_n.38), kind=kOutput, calls=%fused_computation.15 | convolution fusion | flops 440602624 | bytes 14311428 | tf_op jit(solution)/shard_map/dot_general | solution.py:114
  114.5 7.0 %fusion.43 = f32[256,2,2,256]{0,3,2,1:T(8,128)} fusion(bf16[2048,2,256,1]{0,2,3,1:T(8,128)(2,1)S(1)} %copy.73, f32[2,2048,256,2]{2,1,3,0:T(8,128)} %copy-done.4, f32[2,2,256]{2,1,0:T(2,128)S(1)} %get-tuple-element.30, pred[256,2048]{0,1:T(8,128)(4,1)S(1)} %copy-done.10, f32[256,2,2]{0,2,1:T(2,128)S(1)} %get-tuple-element.9), kind=kOutput, calls=%fused_computation.50 | convolution fusion | flops 1084489728 | bytes 12066816 | tf_op jit(solution)/shard_map/hgrk,khd->hgrd/dot_general | solution.py:37
  121.6 2.5 fusion.47
  124.4 2.6 reshape.318
  127.1 1.6 fusion.1
  128.7 3.2 %copy-done.3 = f32[2,2048,256,2]{2,1,3,0:T(8,128)} copy-done((f32[2,2048,256,2]{2,1,3,0:T(8,128)}, f32[2,2048,256,2]{2,1,3,0:T(8,128)S(1)}, u32[]{:S(2)}) %copy-start.3) | copy-done | bytes 8388632
  131.9 2.1 fusion.4
  134.7 4.0 %reshape.319 = bf16[2048,2,256]{2,1,0:T(2,128)(2,1)} reshape(bf16[2048,512]{1,0:T(8,128)(2,1)} %all-gather.15.cloned.1.call-done) | data formatting | bytes 4194304 | tf_op jit(solution)/shard_map/reshape | solution.py:29
  138.7 4.7 %copy.83 = bf16[2048,2,256,1]{0,2,3,1:T(8,128)(2,1)S(1)} copy(bf16[2048,2,256,1]{2,1,0,3:T(2,128)(2,1)} %bitcast.249) | data formatting | bytes 4194304 | tf_op jit(solution)/shard_map/reshape | solution.py:29
  143.4 29.2 %all-reduce.3.cloned.1.call-done = bf16[32,3584]{1,0:T(8,128)(2,1)} async-done(((bf16[32,3584]{1,0:T(8,128)(2,1)}), bf16[32,3584]{1,0:T(8,128)(2,1)}) %all-reduce.3.cloned.1.call-update) | async-done | bytes 229392 | tf_op jit(solution)/shard_map/psum | solution.py:115
  172.7 1.2 fusion.83
  173.9 3.0 convolution_convert_fusion.11
  176.9 2.8 convolution_convert_fusion.10
  180.1 5.0 %fusion.40 = f32[256,2,2,256]{0,3,2,1:T(8,128)S(1)} fusion(bf16[2048,2,256,1]{0,2,3,1:T(8,128)(2,1)S(1)} %copy.83, f32[2,2048,256,2]{2,1,3,0:T(8,128)} %copy-done.3, f32[2,2,256]{2,1,0:T(2,128)S(1)} %get-tuple-element.22, pred[256,2048]{0,1:T(8,128)(4,1)S(1)} %copy-done.9, f32[256,2,2]{0,2,1:T(2,128)S(1)} %get-tuple-element.12), kind=kOutput, calls=%fused_computation.49 | convolution fusion | flops 1084489728 | bytes 12066816 | tf_op jit(solution)/shard_map/hgrk,khd->hgrd/dot_general | solution.py:37
  185.1 1.1 fusion.46
  186.3 4.1 %fusion.158 = (bf16[1,256,3584]{2,1,0:T(8,128)(2,1)}, bf16[1,256,3584]{2,1,0:T(8,128)(2,1)}) fusion(bf16[2,256,3584]{2,1,0:T(8,128)(2,1)} %param.9), kind=kLoop, calls=%fused_computation.195 | loop fusion | bytes 7340032 | tf_op jit(solution)/shard_map/slice | solution.py:61
  190.4 4.5 %convolution_convert_fusion.8 = bf16[32,1024]{1,0:T(8,128)(2,1)S(1)} fusion(bf16[3584,1024]{1,0:T(8,128)(2,1)} %param.13, bf16[32,3584]{1,0:T(8,128)(2,1)S(1)} %copy-done.8, f32[32]{0:T(128)S(1)} %add_rsqrt_fusion.2, f32[3584]{0:T(1024)S(1)} %convert_element_type.159), kind=kOutput, calls=%fused_computation.85 | convolution fusion | flops 235372544 | bytes 7649408 | tf_op jit(solution)/shard_map/dot_general | solution.py:74
  195.2 2.4 fusion.164
  198.2 0.8 fusion.63
  199.1 16.7 %all_gather.31 = bf16[32,4096]{1,0:T(8,128)(2,1)S(1)} all-gather(bf16[32,1024]{1,0:T(8,128)(2,1)S(1)} %convert_element_type.204), channel_id=1, replica_groups=mesh['seq'=8,'head'=4] {'head'}, dimensions={1}, use_global_device_ids=true | all-gather | bytes 327680 | tf_op jit(solution)/shard_map/all_gather | solution.py:106
  215.8 8.0 %convolution_convert_fusion = bf16[32,3584]{1,0:T(8,128)(2,1)} fusion(bf16[896,3584]{1,0:T(8,128)(2,1)} %param.17, bf16[32,4096]{1,0:T(8,128)(2,1)S(1)} %all_gather.31, bf16[4096,896]{1,0:T(8,128)(2,1)} %param.16, bf16[32,3584]{1,0:T(8,128)(2,1)S(1)} %copy-done.8, s32[]{:T(128)S(6)} %select_n.38), kind=kOutput, calls=%fused_computation.14 | convolution fusion | flops 440602624 | bytes 14311428 | tf_op jit(solution)/shard_map/dot_general | solution.py:114
  223.8 6.1 %fusion.51 = bf16[1,256,896]{2,1,0:T(8,128)(2,1)S(1)} fusion(bf16[256,4096]{0,1:T(8,128)(2,1)} %all-gather.11.cloned.1.call-done, bf16[4096,896]{1,0:T(8,128)(2,1)} %param.16, bf16[1,256,3584]{2,1,0:T(8,128)(2,1)} %get-tuple-element.16, s32[]{:T(128)S(6)} %select_n.38), kind=kOutput, calls=%fused_computation.60 | convolution fusion | flops 1879736320 | bytes 10354692 | tf_op jit(solution)/shard_map/dot_general | solution.py:100
  230.0 40.4 %all-gather.17.cloned.1.call-done = bf16[256,4096]{0,1:T(8,128)(2,1)} async-done(((bf16[256,1024]{0,1:T(8,128)(2,1)}), bf16[256,4096]{0,1:T(8,128)(2,1)}) %all-gather.17.cloned.1.call-update) | async-done | bytes 2097168 | tf_op jit(solution)/shard_map/all_gather | solution.py:101
  270.4 6.2 %fusion.50 = bf16[1,256,896]{2,1,0:T(8,128)(2,1)S(1)} fusion(bf16[256,4096]{0,1:T(8,128)(2,1)} %all-gather.17.cloned.1.call-done, bf16[4096,896]{1,0:T(8,128)(2,1)} %param.16, bf16[1,256,3584]{2,1,0:T(8,128)(2,1)} %get-tuple-element.17, s32[]{:T(128)S(6)} %select_n.38), kind=kOutput, calls=%fused_computation.59 | convolution fusion | flops 1879736320 | bytes 10354692 | tf_op jit(solution)/shard_map/dot_general | solution.py:100
  276.6 1.0 pad_maximum_fusion
  277.6 29.7 %all-reduce.5.cloned.1.call-done = bf16[32,3584]{1,0:T(8,128)(2,1)} async-done(((bf16[32,3584]{1,0:T(8,128)(2,1)}), bf16[32,3584]{1,0:T(8,128)(2,1)}) %all-reduce.5.cloned.1.call-update) | async-done | bytes 229392 | tf_op jit(solution)/shard_map/psum | solution.py:115
  307.3 1.6 copy.195
  (106 shorter events, 7.8 us)
Async XLA Ops:
  7.2 41.2 %all-gather.7.cloned.1.call-start = ((), (), s32[]{:S(2)}) async-start(), calls=%async_computation | async-start | bytes 2359296 | tf_op jit(solution)/shard_map/all_gather | solution.py:87
  7.2 3.9 %copy-start = (bf16[2,256,3584]{2,1,0:T(8,128)(2,1)S(1)}, bf16[2,256,3584]{2,1,0:T(8,128)(2,1)}, u32[]{:S(2)}) copy-start(bf16[2,256,3584]{2,1,0:T(8,128)(2,1)} %param.9) | copy-start | bytes 11010052
  15.1 60.4 %all-gather.9.cloned.1.call-start = ((), (), s32[]{:S(2)}) async-start(), calls=%async_computation.1 | async-start | bytes 2359296 | tf_op jit(solution)/shard_map/all_gather | solution.py:88
  19.6 104.8 %all-gather.13.cloned.1.call-start = ((), (), s32[]{:S(2)}) async-start(), calls=%async_computation.4 | async-start | bytes 2359296 | tf_op jit(solution)/shard_map/all_gather | solution.py:87
  24.2 5.0 %copy-start.7 = (bf16[32,3584]{1,0:T(8,128)(2,1)S(1)}, bf16[32,3584]{1,0:T(8,128)(2,1)}, u32[]{:S(2)}) copy-start(bf16[32,3584]{1,0:T(8,128)(2,1)} %param.11) | copy-start | bytes 688132
  24.2 110.5 %all-gather.15.cloned.1.call-start = ((), (), s32[]{:S(2)}) async-start(), calls=%async_computation.5 | async-start | bytes 2359296 | tf_op jit(solution)/shard_map/all_gather | solution.py:88
  29.0 143.7 %all-reduce.3.cloned.1.call-start = ((), (), s32[]{:S(2)}) async-start(), calls=%async_computation.3 | async-start | bytes 458752 | tf_op jit(solution)/shard_map/psum | solution.py:115
  29.2 3.2 %copy-start.2 = (bf16[3584,512]{1,0:T(8,128)(2,1)S(1)}, bf16[3584,512]{1,0:T(8,128)(2,1)}, u32[]{:S(2)}) copy-start(bf16[3584,512]{1,0:T(8,128)(2,1)} %param.15) | copy-start | bytes 11010052
  29.4 8.6 %slice-start = ((s8[7340032]{0:T(1024)(128)(4,1)}), s8[4194304]{0:T(1024)(128)(4,1)S(1)}, s32[]{:S(2)}) async-start(s8[7340032]{0:T(1024)(128)(4,1)} %bitcast.242), calls=%async_computation.8 | async-start | bytes 8388608
  32.4 5.6 %slice-start.1 = ((s8[7340032]{0:T(1024)(128)(4,1)}), s8[3145728]{0:T(1024)(128)(4,1)S(1)}, s32[]{:S(2)}) async-start(s8[7340032]{0:T(1024)(128)(4,1)} %bitcast.242), calls=%async_computation.9 | async-start | bytes 6291456
  33.2 5.0 %copy-start.1 = (bf16[2,256,3584]{2,1,0:T(8,128)(2,1)S(1)}, bf16[2,256,3584]{2,1,0:T(8,128)(2,1)}, u32[]{:S(2)}) copy-start(bf16[2,256,3584]{2,1,0:T(8,128)(2,1)} %param.9) | copy-start | bytes 11010052
  40.4 2.3 copy-start.21
  43.0 7.9 %copy-start.12 = (bf16[256,2,2,256]{3,2,1,0:T(2,128)(2,1)}, bf16[256,2,2,256]{3,2,1,0:T(2,128)(2,1)S(1)}, u32[]{:S(2)}) copy-start(bf16[256,2,2,256]{3,2,1,0:T(2,128)(2,1)S(1)} %reshape.310) | copy-start | bytes 1572868
  43.2 5.1 %copy-start.17 = (f32[2,2,32]{2,1,0:T(2,128)}, f32[2,2,32]{2,1,0:T(2,128)S(1)}, u32[]{:S(2)}) copy-start(f32[2,2,32]{2,1,0:T(2,128)S(1)} %get-tuple-element.26) | copy-start | bytes 1540
  43.5 4.8 %copy-start.13 = (f32[2,2,256,32]{2,3,1,0:T(8,128)}, f32[2,2,256,32]{2,3,1,0:T(8,128)S(1)}, u32[]{:S(2)}) copy-start(f32[2,2,256,32]{2,3,1,0:T(8,128)S(1)} %get-tuple-element.33) | copy-start | bytes 393220
  43.5 4.8 %copy-start.15 = (f32[2,2,256]{2,1,0:T(2,128)}, f32[2,2,256]{2,1,0:T(2,128)S(1)}, u32[]{:S(2)}) copy-start(f32[2,2,256]{2,1,0:T(2,128)S(1)} %get-tuple-element.32) | copy-start | bytes 12292
  50.9 28.5 %copy-start.6 = (bf16[2048,2,256]{2,1,0:T(2,128)(2,1)}, bf16[2048,2,256]{2,1,0:T(2,128)(2,1)S(1)}, u32[]{:S(2)}) copy-start(bf16[2048,2,256]{2,1,0:T(2,128)(2,1)S(1)} %reshape.312) | copy-start | bytes 6291460
  52.4 31.8 %copy-start.19 = (f32[2,2,32]{2,1,0:T(2,128)S(1)}, f32[2,2,32]{2,1,0:T(2,128)}, u32[]{:S(2)}) copy-start(f32[2,2,32]{2,1,0:T(2,128)} %get-tuple-element.24) | copy-start | bytes 1540
  79.4 5.1 %copy-start.18 = (f32[2,2,32]{2,1,0:T(2,128)S(1)}, f32[2,2,32]{2,1,0:T(2,128)}, u32[]{:S(2)}) copy-start(f32[2,2,32]{2,1,0:T(2,128)} %copy-done.17) | copy-start | bytes 1540
  79.4 5.1 %copy-start.22 = (f32[2,2,32]{2,1,0:T(2,128)S(1)}, f32[2,2,32]{2,1,0:T(2,128)}, u32[]{:S(2)}) copy-start(f32[2,2,32]{2,1,0:T(2,128)} %fusion.96) | copy-start | bytes 1540
  99.7 3.5 %copy-start.10 = (pred[256,2048]{0,1:T(8,128)(4,1)S(1)}, pred[256,2048]{0,1:T(8,128)(4,1)}, u32[]{:S(2)}) copy-start(pred[256,2048]{0,1:T(8,128)(4,1)} %get-tuple-element.20) | copy-start | bytes 1572868
  103.3 3.2 %copy-start.4 = (f32[2,2048,256,2]{2,1,3,0:T(8,128)}, f32[2,2048,256,2]{2,1,3,0:T(8,128)S(1)}, u32[]{:S(2)}) copy-start(f32[2,2048,256,2]{2,1,3,0:T(8,128)S(1)} %get-tuple-element.31) | copy-start | bytes 25165828
  103.3 3.2 %copy-start.16 = (f32[2,2,256]{2,1,0:T(2,128)S(1)}, f32[2,2,256]{2,1,0:T(2,128)}, u32[]{:S(2)}) copy-start(f32[2,2,256]{2,1,0:T(2,128)} %copy-done.15) | copy-start | bytes 12292
  103.3 3.2 %copy-start.20 = (f32[2,2,256]{2,1,0:T(2,128)S(1)}, f32[2,2,256]{2,1,0:T(2,128)}, u32[]{:S(2)}) copy-start(f32[2,2,256]{2,1,0:T(2,128)} %fusion.86) | copy-start | bytes 12292
  114.5 7.1 %copy-start.14 = (f32[2,2,256,32]{2,3,1,0:T(8,128)S(1)}, f32[2,2,256,32]{2,3,1,0:T(8,128)}, u32[]{:S(2)}) copy-start(f32[2,2,256,32]{2,3,1,0:T(8,128)} %copy-done.13) | copy-start | bytes 393220
  121.5 102.3 %all-gather.11.cloned.1.call-start = ((), (), s32[]{:S(2)}) async-start(), calls=%async_computation.2 | async-start | bytes 2621440 | tf_op jit(solution)/shard_map/all_gather | solution.py:101
  121.6 5.5 %copy-start.9 = (pred[256,2048]{0,1:T(8,128)(4,1)S(1)}, pred[256,2048]{0,1:T(8,128)(4,1)}, u32[]{:S(2)}) copy-start(pred[256,2048]{0,1:T(8,128)(4,1)} %get-tuple-element.21) | copy-start | bytes 1572868
  121.6 5.5 %copy-start.11 = (bf16[256,2,2,256]{3,2,1,0:T(2,128)(2,1)S(1)}, bf16[256,2,2,256]{3,2,1,0:T(2,128)(2,1)}, u32[]{:S(2)}) copy-start(bf16[256,2,2,256]{3,2,1,0:T(2,128)(2,1)} %reshape.316) | copy-start | bytes 1572868
  124.1 146.3 %all-gather.17.cloned.1.call-start = ((), (), s32[]{:S(2)}) async-start(), calls=%async_computation.6 | async-start | bytes 2621440 | tf_op jit(solution)/shard_map/all_gather | solution.py:101
  127.0 1.6 copy-start.5
  128.7 3.2 %copy-start.3 = (f32[2,2048,256,2]{2,1,3,0:T(8,128)}, f32[2,2048,256,2]{2,1,3,0:T(8,128)S(1)}, u32[]{:S(2)}) copy-start(f32[2,2048,256,2]{2,1,3,0:T(8,128)S(1)} %get-tuple-element.23) | copy-start | bytes 25165828
  172.7 4.2 %copy-start.8 = (bf16[32,3584]{1,0:T(8,128)(2,1)S(1)}, bf16[32,3584]{1,0:T(8,128)(2,1)}, u32[]{:S(2)}) copy-start(bf16[32,3584]{1,0:T(8,128)(2,1)} %all-reduce.3.cloned.1.call-done) | copy-start | bytes 688132
  186.2 121.1 %all-reduce.5.cloned.1.call-start = ((), (), s32[]{:S(2)}) async-start(), calls=%async_computation.7 | async-start | bytes 458752 | tf_op jit(solution)/shard_map/psum | solution.py:115
Sparse Core Ops, SparseCore 0:
  15.2 30.4 all-gather.6
  47.6 27.7 all-gather.8
  77.3 27.7 all-gather.12
  106.9 27.7 all-gather.14
  137.4 35.1 all-reduce.2
  174.1 49.5 all-gather.10
  225.9 44.4 all-gather.16
  273.3 33.9 all-reduce.4
where the time goes:
time: 317 us; the launch traced here: 316 us
  waiting for transfers between devices  123 us (39%)
  matrix products  96.5 us (30%)
  local copies, waits for them, and re-layouts  34.9 us (11%)
  blocking collectives  30.8 us (10%)
  other arithmetic  14.7 us (5%)
  between operations  14.7 us (5%)
    psum x2, waiting for transfers between devices, per_device(): mem = lax.psum(partial_mem.astype(jnp.bfloat16), 'head')  59 us
    all_gather x2, waiting for transfers between devices, per_device(): lax.all_gather(attn_tok, 'head', axis=1, tiled=True)  40.4 us
    all_gather x2, blocking collectives, per_device(): lax.all_gather(attn_mem, 'head', axis=1, tiled=True)  30.8 us
    all_gather x2, waiting for transfers between devices, per_device(): lax.all_gather(values, 'seq', axis=0, tiled=True)  23.8 us
    dot_general x8, matrix products, partial_block(): jnp.einsum('hgrk,khd->hgrd', weights.astype(jnp.bfloat16), value_heads, p...  17.6 us
    reshape x6, local copies, waits for them, and re-layouts, partial_block(): value_heads = values.reshape(values.shape[0], -1, HD)  17.5 us
    dot_general x2, matrix products, per_device(): partial_mem = jnp.dot(mem_out, mem_proj, preferred_element_type=jnp.float32)  16 us
    dot_general x2, matrix products, per_device(): jnp.dot(lax.all_gather(attn_tok, 'head', axis=1, tiled=True), w_out, pref...  12.3 us
  transfers between devices with their start and end apart: 8, of which 5 were waited for; matrix products, arithmetic and copies ran while one was open for 42% of the time, Pallas kernels for 0%

commit v1 on v0

--- a/solution.py
+++ b/solution.py
@@ -112,7 +112,9 @@
         mem_cols = lax.dynamic_slice_in_dim(mem, col_start, columns, 1).astype(jnp.float32)
         mem_out = (mem_cols + out_mem).astype(jnp.bfloat16)
         partial_mem = jnp.dot(mem_out, mem_proj, preferred_element_type=jnp.float32)
-        mem = lax.psum(partial_mem.astype(jnp.bfloat16), "head")
+        part = partial_mem.astype(jnp.bfloat16)
+        parts = lax.all_gather(part, "head")
+        mem = jnp.sum(parts, axis=0)
     return (jnp.stack(outputs, axis=0), mem)
 
 

time: 317 us -> 263 us (0.83)
  waiting for transfers between devices: 123 us -> 41.1 us
  blocking collectives: 30.8 us -> 73.6 us
  matrix products: 96.5 us -> 86.5 us
  local copies, waits for them, and re-layouts: 34.9 us -> 30 us
    psum x2 -> x0, waiting for transfers between devices: 59 us -> none  [per_device(): mem = lax.psum(partial_mem.astype(jnp.bfloat16), 'head')]
    all_gather x0 -> x2, blocking collectives: none -> 43.4 us  [per_device(): parts = lax.all_gather(part, 'head')]
    all_gather x2, waiting for transfers between devices: 40.4 us -> 19.7 us  [per_device(): lax.all_gather(attn_tok, 'head', axis=1, tiled=True)]
    dot_general x8, matrix products: 17.6 us -> 8.93 us  [partial_block(): jnp.einsum('hgrk,khd->hgrd', weights.astype(jnp.bfloat16), value_heads, p...]
    unnamed x51 -> x62, local copies, waits for them, and re-layouts: 6.22 us -> 1.29 us
  transfers between devices with their start and end apart: 8 -> 6, of which waited for: 5 -> 2; matrix products, arithmetic and copies ran while one was open for 42% -> 44% of each run, Pallas kernels for 0% -> 0%
where the time goes in v1:
time: 263 us; the launch traced here: 262 us
  matrix products  86.5 us (33%)
  blocking collectives  73.6 us (28%)
  waiting for transfers between devices  41.1 us (16%)
  local copies, waits for them, and re-layouts  30 us (11%)
  other arithmetic  15.3 us (6%)
  between operations  14.7 us (6%)
    all_gather x2, blocking collectives, per_device(): parts = lax.all_gather(part, 'head')  43.4 us
    all_gather x2, blocking collectives, per_device(): lax.all_gather(attn_mem, 'head', axis=1, tiled=True)  30.2 us
    all_gather x2, waiting for transfers between devices, per_device(): lax.all_gather(values, 'seq', axis=0, tiled=True)  21.2 us
    all_gather x2, waiting for transfers between devices, per_device(): lax.all_gather(attn_tok, 'head', axis=1, tiled=True)  19.7 us
    reshape x6, local copies, waits for them, and re-layouts, partial_block(): value_heads = values.reshape(values.shape[0], -1, HD)  18.2 us
    dot_general x2, matrix products, per_device(): partial_mem = jnp.dot(mem_out, mem_proj, preferred_element_type=jnp.float32)  15.4 us
    dot_general x2, matrix products, per_device(): jnp.dot(lax.all_gather(attn_tok, 'head', axis=1, tiled=True), w_out, pref...  12.4 us
    dot_general x8, matrix products, partial_block(): jnp.einsum('rhgd,khd->hgrk', query, key_heads, preferred_element_type=jnp...  11.2 us
  transfers between devices with their start and end apart: 6, of which 2 were waited for; matrix products, arithmetic and copies ran while one was open for 44% of the time, Pallas kernels for 0%

profile of v1, /device:TPU:0, one launch (start us, length us, event | category | flops | bytes accessed | tf_op | source)
XLA Modules:
  0.0 261.8 jit_solution(6723832080244002121)
XLA Ops:
  7.2 0.9 convert_element_type.163
  8.1 3.0 %fusion.12 = (f32[256]{0:T(256)S(1)}, f32[256]{0:T(256)S(1)}) fusion(bf16[2,256,3584]{2,1,0:T(8,128)(2,1)} %param.9), kind=kLoop, calls=%fused_computation.20 | loop fusion | flops 5504512 | bytes 3672064 | tf_op jit(solution)/shard_map/reduce_sum | solution.py:11
  11.1 3.9 %convolution_convert_fusion.7 = bf16[256,512]{1,0:T(8,128)(2,1)} fusion(bf16[3584,512]{1,0:T(8,128)(2,1)} %param.14, f32[3584]{0:T(1024)S(1)} %convert_element_type.163, f32[256]{0:T(256)S(1)} %add_rsqrt_fusion.1, bf16[2,256,3584]{2,1,0:T(8,128)(2,1)S(1)} %copy-done), kind=kOutput, calls=%fused_computation.64 | convolution fusion | flops 943325184 | bytes 5784576 | tf_op jit(solution)/shard_map/dot_general | solution.py:71
  15.1 4.5 %convolution_convert_fusion.6 = bf16[256,512]{1,0:T(8,128)(2,1)} fusion(bf16[3584,512]{1,0:T(8,128)(2,1)} %param.15, f32[3584]{0:T(1024)S(1)} %convert_element_type.163, f32[256]{0:T(256)S(1)} %add_rsqrt_fusion.1, bf16[2,256,3584]{2,1,0:T(8,128)(2,1)} %param.9), kind=kOutput, calls=%fused_computation.63 | convolution fusion | flops 943325184 | bytes 5782528 | tf_op jit(solution)/shard_map/dot_general | solution.py:72
  19.7 4.5 %convolution_convert_fusion.4 = bf16[256,512]{1,0:T(8,128)(2,1)} fusion(bf16[3584,512]{1,0:T(8,128)(2,1)} %param.15, f32[256]{0:T(256)S(1)} %add_rsqrt_fusion, f32[3584]{0:T(1024)S(1)} %convert_element_type.163, bf16[2,256,3584]{2,1,0:T(8,128)(2,1)} %param.9), kind=kOutput, calls=%fused_computation.61 | convolution fusion | flops 943325184 | bytes 5782528 | tf_op jit(solution)/shard_map/dot_general | solution.py:72
  24.2 4.7 %convolution_convert_fusion.5 = bf16[256,512]{1,0:T(8,128)(2,1)} fusion(bf16[3584,512]{1,0:T(8,128)(2,1)} %param.14, f32[256]{0:T(256)S(1)} %add_rsqrt_fusion, f32[3584]{0:T(1024)S(1)} %convert_element_type.163, bf16[2,256,3584]{2,1,0:T(8,128)(2,1)} %param.9), kind=kOutput, calls=%fused_computation.62 | convolution fusion | flops 943325184 | bytes 5782528 | tf_op jit(solution)/shard_map/dot_general | solution.py:71
  29.4 3.0 %convolution_convert_fusion.13 = bf16[32,512]{1,0:T(8,128)(2,1)S(1)} fusion(bf16[3584,512]{1,0:T(8,128)(2,1)} %param.14, bf16[32,3584]{1,0:T(8,128)(2,1)S(1)} %copy-done.5, f32[3584]{0:T(1024)S(1)} %convert_element_type.163, f32[32]{0:T(128)S(1)} %add_rsqrt_fusion.3), kind=kOutput, calls=%fused_computation.96 | convolution fusion | flops 117915648 | bytes 3946624 | tf_op jit(solution)/shard_map/dot_general | solution.py:78
  32.4 0.8 convolution_convert_fusion.12
  33.2 4.8 %convolution_convert_fusion.9 = bf16[32,1024]{1,0:T(8,128)(2,1)S(1)} fusion(bf16[3584,1024]{1,0:T(8,128)(2,1)} %param.13, bf16[32,3584]{1,0:T(8,128)(2,1)S(1)} %copy-done.5, f32[3584]{0:T(1024)S(1)} %convert_element_type.163, f32[32]{0:T(128)S(1)} %add_rsqrt_fusion.3), kind=kOutput, calls=%fused_computation.86 | convolution fusion | flops 235372544 | bytes 7649408 | tf_op jit(solution)/shard_map/dot_general | solution.py:74
  38.2 2.1 convolution_convert_fusion.3
  40.3 2.1 fusion.158
  42.4 2.1 convolution_convert_fusion.2
  45.5 1.2 reshape.316
  47.9 2.3 fusion.21
  50.2 2.6 reshape.312
  52.8 1.4 fusion.160
  54.2 21.2 %all-gather.11.cloned.1.call-done = bf16[2048,512]{1,0:T(8,128)(2,1)} async-done(((bf16[256,512]{1,0:T(8,128)(2,1)}), bf16[2048,512]{1,0:T(8,128)(2,1)}) %all-gather.11.cloned.1.call-update) | async-done | bytes 2097168 | tf_op jit(solution)/shard_map/all_gather | solution.py:88
  75.4 4.0 %reshape.313 = bf16[2048,2,256]{2,1,0:T(2,128)(2,1)} reshape(bf16[2048,512]{1,0:T(8,128)(2,1)} %all-gather.11.cloned.1.call-done) | data formatting | bytes 4194304 | tf_op jit(solution)/shard_map/reshape | solution.py:29
  79.4 4.7 %copy.73 = bf16[2048,2,256,1]{0,2,3,1:T(8,128)(2,1)S(1)} copy(bf16[2048,2,256,1]{2,1,0,3:T(2,128)(2,1)} %bitcast.250) | data formatting | bytes 4194304 | tf_op jit(solution)/shard_map/reshape | solution.py:29
  84.7 0.8 fusion.62
  85.6 13.9 %all_gather.39 = bf16[32,4096]{1,0:T(8,128)(2,1)S(1)} all-gather(bf16[32,1024]{1,0:T(8,128)(2,1)S(1)} %convert_element_type.185), channel_id=1, replica_groups=mesh['seq'=8,'head'=4] {'head'}, dimensions={1}, use_global_device_ids=true | all-gather | bytes 327680 | tf_op jit(solution)/shard_map/all_gather | solution.py:106
  99.5 8.1 %convolution_convert_fusion.1 = bf16[32,3584]{1,0:T(8,128)(2,1)} fusion(bf16[896,3584]{1,0:T(8,128)(2,1)} %param.17, bf16[32,4096]{1,0:T(8,128)(2,1)S(1)} %all_gather.39, bf16[4096,896]{1,0:T(8,128)(2,1)} %param.16, bf16[32,3584]{1,0:T(8,128)(2,1)S(1)} %copy-done.5, s32[]{:T(128)S(6)} %select_n.38), kind=kOutput, calls=%fused_computation.15 | convolution fusion | flops 440602624 | bytes 14311428 | tf_op jit(solution)/shard_map/dot_general | solution.py:114
  107.7 20.4 %all-gather = bf16[128,3584]{1,0:T(8,128)(2,1)S(1)} all-gather(bf16[32,3584]{1,0:T(8,128)(2,1)} %convolution_convert_fusion.1), channel_id=2, replica_groups=mesh['seq'=8,'head'=4] {'head'}, dimensions={0}, use_global_device_ids=true | all-gather | bytes 1146880 | tf_op jit(solution)/shard_map/all_gather | solution.py:116
  128.5 4.6 %convolution_convert_fusion.8 = bf16[32,1024]{1,0:T(8,128)(2,1)S(1)} fusion(bf16[3584,1024]{1,0:T(8,128)(2,1)} %param.13, bf16[32,3584]{1,0:T(8,128)(2,1)S(1)} %reduce_sum.158, f32[32]{0:T(128)S(1)} %add_rsqrt_fusion.2, f32[3584]{0:T(1024)S(1)} %convert_element_type.163), kind=kOutput, calls=%fused_computation.85 | convolution fusion | flops 235372544 | bytes 7649408 | tf_op jit(solution)/shard_map/dot_general | solution.py:74
  133.1 2.9 %convolution_convert_fusion.11 = bf16[32,512]{1,0:T(8,128)(2,1)S(1)} fusion(bf16[3584,512]{1,0:T(8,128)(2,1)} %param.14, bf16[32,3584]{1,0:T(8,128)(2,1)S(1)} %reduce_sum.158, f32[32]{0:T(128)S(1)} %add_rsqrt_fusion.2, f32[3584]{0:T(1024)S(1)} %convert_element_type.163), kind=kOutput, calls=%fused_computation.94 | convolution fusion | flops 117915648 | bytes 3946624 | tf_op jit(solution)/shard_map/dot_general | solution.py:78
  136.1 3.2 %fusion = (f32[2,2,256]{2,1,0:T(2,128)S(1)}, f32[2,2048,256,2]{2,1,3,0:T(8,128)S(1)}) fusion(pred[256,2048]{0,1:T(8,128)(4,1)S(1)} %copy-done.7, bf16[256,2,2,256]{3,2,1,0:T(2,128)(2,1)S(1)} %copy-done.10, bf16[2048,2,256,1]{2,1,0,3:T(2,128)(2,1)} %bitcast.247), kind=kOutput, calls=%fused_computation.4 | convolution fusion | flops 1080032256 | bytes 11538432 | tf_op jit(solution)/shard_map/rhgd,khd->hgrk/dot_general | solution.py:31
  139.3 2.1 fusion.2
  141.6 2.3 fusion.43
  144.0 1.2 fusion.47
  145.2 1.0 copy-done.3
  146.1 0.8 convolution_convert_fusion.10
  148.5 4.0 %reshape.319 = bf16[2048,2,256]{2,1,0:T(2,128)(2,1)} reshape(bf16[2048,512]{1,0:T(8,128)(2,1)} %all-gather.17.cloned.1.call-done) | data formatting | bytes 4194304 | tf_op jit(solution)/shard_map/reshape | solution.py:29
  152.5 4.8 %copy.83 = bf16[2048,2,256,1]{0,2,3,1:T(8,128)(2,1)S(1)} copy(bf16[2048,2,256,1]{2,1,0,3:T(2,128)(2,1)} %bitcast.251) | data formatting | bytes 4194304 | tf_op jit(solution)/shard_map/reshape | solution.py:29
  157.4 4.0 %reshape.318 = bf16[2048,2,256]{2,1,0:T(2,128)(2,1)} reshape(bf16[2048,512]{1,0:T(8,128)(2,1)} %all-gather.15.cloned.1.call-done) | data formatting | bytes 4194304 | tf_op jit(solution)/shard_map/reshape | solution.py:28
  161.7 3.2 %fusion.1 = (f32[2,2,256]{2,1,0:T(2,128)S(1)}, f32[2,2048,256,2]{2,1,3,0:T(8,128)S(1)}) fusion(pred[256,2048]{0,1:T(8,128)(4,1)S(1)} %copy-done.6, bf16[256,2,2,256]{3,2,1,0:T(2,128)(2,1)S(1)} %copy-done.8, bf16[2048,2,256,1]{2,1,0,3:T(2,128)(2,1)} %bitcast.248), kind=kOutput, calls=%fused_computation.5 | convolution fusion | flops 1080032256 | bytes 11538432 | tf_op jit(solution)/shard_map/rhgd,khd->hgrk/dot_general | solution.py:31
  164.9 2.1 fusion.4
  167.1 2.3 fusion.40
  169.4 1.1 fusion.46
  170.6 2.5 fusion.164
  173.6 0.8 fusion.63
  174.5 16.2 %all_gather.45 = bf16[32,4096]{1,0:T(8,128)(2,1)S(1)} all-gather(bf16[32,1024]{1,0:T(8,128)(2,1)S(1)} %convert_element_type.208), channel_id=1, replica_groups=mesh['seq'=8,'head'=4] {'head'}, dimensions={1}, use_global_device_ids=true | all-gather | bytes 327680 | tf_op jit(solution)/shard_map/all_gather | solution.py:106
  190.7 7.3 %convolution_convert_fusion = bf16[32,3584]{1,0:T(8,128)(2,1)S(1)} fusion(bf16[896,3584]{1,0:T(8,128)(2,1)} %param.17, bf16[32,4096]{1,0:T(8,128)(2,1)S(1)} %all_gather.45, bf16[4096,896]{1,0:T(8,128)(2,1)} %param.16, bf16[32,3584]{1,0:T(8,128)(2,1)S(1)} %reduce_sum.158, s32[]{:T(128)S(6)} %select_n.38), kind=kOutput, calls=%fused_computation.14 | convolution fusion | flops 440602624 | bytes 14311428 | tf_op jit(solution)/shard_map/dot_general | solution.py:114
  198.0 23.0 %all-gather.1 = bf16[128,3584]{1,0:T(8,128)(2,1)S(1)} all-gather(bf16[32,3584]{1,0:T(8,128)(2,1)S(1)} %convolution_convert_fusion), channel_id=3, replica_groups=mesh['seq'=8,'head'=4] {'head'}, dimensions={0}, use_global_device_ids=true | all-gather | bytes 1146880 | tf_op jit(solution)/shard_map/all_gather | solution.py:116
  221.0 0.9 reduce_sum.169
  221.8 6.2 %fusion.51 = bf16[1,256,896]{2,1,0:T(8,128)(2,1)S(1)} fusion(bf16[256,4096]{0,1:T(8,128)(2,1)} %all-gather.13.cloned.1.call-done, bf16[4096,896]{1,0:T(8,128)(2,1)} %param.16, bf16[1,256,3584]{2,1,0:T(8,128)(2,1)} %get-tuple-element.16, s32[]{:T(128)S(6)} %select_n.38), kind=kOutput, calls=%fused_computation.60 | convolution fusion | flops 1879736320 | bytes 10354692 | tf_op jit(solution)/shard_map/dot_general | solution.py:100
  228.1 19.7 %all-gather.19.cloned.1.call-done = bf16[256,4096]{0,1:T(8,128)(2,1)} async-done(((bf16[256,1024]{0,1:T(8,128)(2,1)}), bf16[256,4096]{0,1:T(8,128)(2,1)}) %all-gather.19.cloned.1.call-update) | async-done | bytes 2097168 | tf_op jit(solution)/shard_map/all_gather | solution.py:101
  247.8 6.2 %fusion.50 = bf16[1,256,896]{2,1,0:T(8,128)(2,1)S(1)} fusion(bf16[256,4096]{0,1:T(8,128)(2,1)} %all-gather.19.cloned.1.call-done, bf16[4096,896]{1,0:T(8,128)(2,1)} %param.16, bf16[1,256,3584]{2,1,0:T(8,128)(2,1)} %get-tuple-element.17, s32[]{:T(128)S(6)} %select_n.38), kind=kOutput, calls=%fused_computation.59 | convolution fusion | flops 1879736320 | bytes 10354692 | tf_op jit(solution)/shard_map/dot_general | solution.py:100
  254.0 1.0 pad_maximum_fusion
  (115 shorter events, 6.9 us)
Async XLA Ops:
  7.2 43.0 %all-gather.9.cloned.1.call-start = ((), (), s32[]{:S(2)}) async-start(), calls=%async_computation | async-start | bytes 2359296 | tf_op jit(solution)/shard_map/all_gather | solution.py:87
  7.2 3.9 %copy-start = (bf16[2,256,3584]{2,1,0:T(8,128)(2,1)S(1)}, bf16[2,256,3584]{2,1,0:T(8,128)(2,1)}, u32[]{:S(2)}) copy-start(bf16[2,256,3584]{2,1,0:T(8,128)(2,1)} %param.9) | copy-start | bytes 11010052
  15.1 60.4 %all-gather.11.cloned.1.call-start = ((), (), s32[]{:S(2)}) async-start(), calls=%async_computation.1 | async-start | bytes 2359296 | tf_op jit(solution)/shard_map/all_gather | solution.py:88
  19.6 128.9 %all-gather.17.cloned.1.call-start = ((), (), s32[]{:S(2)}) async-start(), calls=%async_computation.4 | async-start | bytes 2359296 | tf_op jit(solution)/shard_map/all_gather | solution.py:88
  24.2 5.0 %copy-start.5 = (bf16[32,3584]{1,0:T(8,128)(2,1)S(1)}, bf16[32,3584]{1,0:T(8,128)(2,1)}, u32[]{:S(2)}) copy-start(bf16[32,3584]{1,0:T(8,128)(2,1)} %param.11) | copy-start | bytes 688132
  24.2 133.2 %all-gather.15.cloned.1.call-start = ((), (), s32[]{:S(2)}) async-start(), calls=%async_computation.3 | async-start | bytes 2359296 | tf_op jit(solution)/shard_map/all_gather | solution.py:87
  29.0 192.9 %all-gather.13.cloned.1.call-start = ((), (), s32[]{:S(2)}) async-start(), calls=%async_computation.2 | async-start | bytes 2621440 | tf_op jit(solution)/shard_map/all_gather | solution.py:101
  29.2 3.2 %copy-start.2 = (bf16[3584,512]{1,0:T(8,128)(2,1)S(1)}, bf16[3584,512]{1,0:T(8,128)(2,1)}, u32[]{:S(2)}) copy-start(bf16[3584,512]{1,0:T(8,128)(2,1)} %param.15) | copy-start | bytes 11010052
  29.4 8.6 %slice-start = ((s8[7340032]{0:T(1024)(128)(4,1)}), s8[4194304]{0:T(1024)(128)(4,1)S(1)}, s32[]{:S(2)}) async-start(s8[7340032]{0:T(1024)(128)(4,1)} %bitcast.244), calls=%async_computation.6 | async-start | bytes 8388608
  32.4 5.6 %slice-start.1 = ((s8[7340032]{0:T(1024)(128)(4,1)}), s8[3145728]{0:T(1024)(128)(4,1)S(1)}, s32[]{:S(2)}) async-start(s8[7340032]{0:T(1024)(128)(4,1)} %bitcast.244), calls=%async_computation.7 | async-start | bytes 6291456
  33.2 5.0 %copy-start.1 = (bf16[2,256,3584]{2,1,0:T(8,128)(2,1)S(1)}, bf16[2,256,3584]{2,1,0:T(8,128)(2,1)}, u32[]{:S(2)}) copy-start(bf16[2,256,3584]{2,1,0:T(8,128)(2,1)} %param.9) | copy-start | bytes 11010052
  42.4 2.2 copy-start.24
  44.6 39.9 %copy-start.13 = (bf16[32,2,256]{2,1,0:T(2,128)(2,1)}, bf16[32,2,256]{2,1,0:T(2,128)(2,1)S(1)}, u32[]{:S(2)}) copy-start(bf16[32,2,256]{2,1,0:T(2,128)(2,1)S(1)} %reshape.311) | copy-start | bytes 98308
  45.0 7.7 %copy-start.9 = (bf16[256,2,2,256]{3,2,1,0:T(2,128)(2,1)}, bf16[256,2,2,256]{3,2,1,0:T(2,128)(2,1)S(1)}, u32[]{:S(2)}) copy-start(bf16[256,2,2,256]{3,2,1,0:T(2,128)(2,1)S(1)} %reshape.310) | copy-start | bytes 1572868
  45.2 4.9 %copy-start.20 = (f32[2,2,32]{2,1,0:T(2,128)}, f32[2,2,32]{2,1,0:T(2,128)S(1)}, u32[]{:S(2)}) copy-start(f32[2,2,32]{2,1,0:T(2,128)S(1)} %get-tuple-element.26) | copy-start | bytes 1540
  45.5 4.7 %copy-start.11 = (f32[2,2,256,32]{2,3,1,0:T(8,128)}, f32[2,2,256,32]{2,3,1,0:T(8,128)S(1)}, u32[]{:S(2)}) copy-start(f32[2,2,256,32]{2,3,1,0:T(8,128)S(1)} %get-tuple-element.33) | copy-start | bytes 393220
  45.5 4.6 %copy-start.16 = (f32[2,2,256]{2,1,0:T(2,128)}, f32[2,2,256]{2,1,0:T(2,128)S(1)}, u32[]{:S(2)}) copy-start(f32[2,2,256]{2,1,0:T(2,128)S(1)} %get-tuple-element.32) | copy-start | bytes 12292
  52.8 26.6 %copy-start.4 = (bf16[2048,2,256]{2,1,0:T(2,128)(2,1)}, bf16[2048,2,256]{2,1,0:T(2,128)(2,1)S(1)}, u32[]{:S(2)}) copy-start(bf16[2048,2,256]{2,1,0:T(2,128)(2,1)S(1)} %reshape.312) | copy-start | bytes 6291460
  54.2 29.9 %copy-start.22 = (f32[2,2,32]{2,1,0:T(2,128)S(1)}, f32[2,2,32]{2,1,0:T(2,128)}, u32[]{:S(2)}) copy-start(f32[2,2,32]{2,1,0:T(2,128)} %get-tuple-element.24) | copy-start | bytes 1540
  79.4 5.1 %copy-start.21 = (f32[2,2,32]{2,1,0:T(2,128)S(1)}, f32[2,2,32]{2,1,0:T(2,128)}, u32[]{:S(2)}) copy-start(f32[2,2,32]{2,1,0:T(2,128)} %copy-done.20) | copy-start | bytes 1540
  79.4 5.1 %copy-start.26 = (f32[2,2,32]{2,1,0:T(2,128)S(1)}, f32[2,2,32]{2,1,0:T(2,128)}, u32[]{:S(2)}) copy-start(f32[2,2,32]{2,1,0:T(2,128)} %fusion.96) | copy-start | bytes 1540
  128.4 4.6 %copy-start.27 = (f32[32]{0:T(128)}, f32[32]{0:T(128)S(1)}, u32[]{:S(2)}) copy-start(f32[32]{0:T(128)S(1)} %add_rsqrt_fusion.2) | copy-start | bytes 388
  133.0 3.0 %copy-start.7 = (pred[256,2048]{0,1:T(8,128)(4,1)S(1)}, pred[256,2048]{0,1:T(8,128)(4,1)}, u32[]{:S(2)}) copy-start(pred[256,2048]{0,1:T(8,128)(4,1)} %get-tuple-element.20) | copy-start | bytes 1572868
  133.0 3.0 %copy-start.10 = (bf16[256,2,2,256]{3,2,1,0:T(2,128)(2,1)S(1)}, bf16[256,2,2,256]{3,2,1,0:T(2,128)(2,1)}, u32[]{:S(2)}) copy-start(bf16[256,2,2,256]{3,2,1,0:T(2,128)(2,1)} %copy-done.9) | copy-start | bytes 1572868
  139.2 2.1 copy-start.17
  139.2 2.1 copy-start.23
  141.6 5.7 %copy-start.18 = (f32[2,2,32]{2,1,0:T(2,128)}, f32[2,2,32]{2,1,0:T(2,128)S(1)}, u32[]{:S(2)}) copy-start(f32[2,2,32]{2,1,0:T(2,128)S(1)} %get-tuple-element.36) | copy-start | bytes 1540
  141.6 2.3 copy-start.12
  141.6 2.3 copy-start.14
  143.9 2.2 copy-start.3
  143.9 2.2 copy-start.28
  147.0 100.8 %all-gather.19.cloned.1.call-start = ((), (), s32[]{:S(2)}) async-start(), calls=%async_computation.5 | async-start | bytes 2621440 | tf_op jit(solution)/shard_map/all_gather | solution.py:101
  152.5 8.8 %copy-start.8 = (bf16[256,2,2,256]{3,2,1,0:T(2,128)(2,1)S(1)}, bf16[256,2,2,256]{3,2,1,0:T(2,128)(2,1)}, u32[]{:S(2)}) copy-start(bf16[256,2,2,256]{3,2,1,0:T(2,128)(2,1)} %reshape.316) | copy-start | bytes 1572868
  152.5 9.2 %copy-start.6 = (pred[256,2048]{0,1:T(8,128)(4,1)S(1)}, pred[256,2048]{0,1:T(8,128)(4,1)}, u32[]{:S(2)}) copy-start(pred[256,2048]{0,1:T(8,128)(4,1)} %get-tuple-element.21) | copy-start | bytes 1572868
  167.0 2.3 copy-start.15
  169.4 4.0 %copy-start.19 = (f32[2,2,32]{2,1,0:T(2,128)S(1)}, f32[2,2,32]{2,1,0:T(2,128)}, u32[]{:S(2)}) copy-start(f32[2,2,32]{2,1,0:T(2,128)} %copy-done.18) | copy-start | bytes 1540
  169.4 3.9 %copy-start.25 = (f32[2,2,32]{2,1,0:T(2,128)S(1)}, f32[2,2,32]{2,1,0:T(2,128)}, u32[]{:S(2)}) copy-start(f32[2,2,32]{2,1,0:T(2,128)} %fusion.98) | copy-start | bytes 1540
Sparse Core Ops, SparseCore 0:
  15.2 30.4 all-gather.8
  47.6 27.7 all-gather.10
  77.3 27.7 all-gather.16
  106.9 27.7 all-gather.14
  147.1 49.6 all-gather.12
  198.7 48.9 all-gather.18
